TPU v7x, 32 devices: a whole 2x2x4 slice. The times are simulated.
32 devices in a mesh: gx: 4 (over x, core), gy: 4 (over z), gz: 2 (over y).
Axes of the slice: x: 2, y: 2, z: 4, core: 2. Of those that a mesh axis runs over, the one named last changes fastest.
Arguments:
- layer_input: bfloat16 [1024, 4096], P('gz', ('gx', 'gy')), may hold values from -6 to 6
- modality: int32 [1024], P('gz'), may hold values 0 or 1
- image_spans: int32 [2, 8], replicated, may hold values from 0 to 1024, as said below
- norm_gain: float32 [2, 4096], P(None, ('gx', 'gy')), may hold values from 0.1 to 1.9
- w_qkv: bfloat16 [3, 4096, 2048], P(None, 'gz', ('gx', 'gy')), as said below
- w_out: bfloat16 [2048, 4096], P(('gx', 'gy'), 'gz'), may hold values from -0.125 to 0.125
- grad_out: bfloat16 [1024, 4096], P('gz', ('gx', 'gy')), may hold values from -6 to 6
Outputs:
- attn_out: bfloat16 [1024, 4096], P('gz', ('gx', 'gy'))
- grad_in: bfloat16 [1024, 4096], P('gz', ('gx', 'gy'))
- grad_qkv: float32 [3, 4096, 2048], P(None, 'gz', ('gx', 'gy'))
- grad_wout: float32 [2048, 4096], P(('gx', 'gy'), 'gz')
- grad_gain: float32 [2, 4096], P(None, ('gx', 'gy'))
Inputs may be any that keep to these rules, and one draw needn't show every extreme that they name: `image_spans`: row 0 holds the first position of each of 8 image spans, in increasing order, and row 1 one past its last; spans are disjoint and none is empty. `w_qkv`: entries are at most 20 * 4096 ** -0.5 in magnitude.
All inputs are finite; a program needn't handle non-finite values. No bound on the sum of `modality` on one device may be relied on, other than what follows from the above.
Results may differ from a plain program's by a relative error of at most 0.035.
The roundings to bfloat16 on the way count: a program that leaves them out, or rounds other values in their place, can miss the bound.
Values may be sent and summed in bfloat16 or wider, within the bound.
A program may use at most 128 MiB of HBM per device.

v0:
```python
import math
import jax
import jax.numpy as jnp
from jax import lax
from jax.sharding import PartitionSpec as P

epsilon = 1e-05
masked_low = -1e30


def span_index(positions, image_spans):
    inside = (positions[:, None] >= image_spans[0][None, :]) & (
        positions[:, None] < image_spans[1][None, :]
    )
    labels = jnp.arange(1, image_spans.shape[1] + 1, dtype=jnp.int32)
    return jnp.sum(jnp.where(inside, labels[None, :], 0), axis=1) - 1


def visible(query_pos, query_span, key_pos, key_span):
    causal = key_pos[None, :] <= query_pos[:, None]
    same_image = (query_span[:, None] == key_span[None, :]) & (query_span[:, None] >= 0)
    return causal | same_image


def per_device(layer_input, modality, image_spans, norm_gain, w_qkv, w_out, grad_out):
    tok_rows, local_width = layer_input.shape
    full_width = local_width * lax.axis_size(("gx", "gy"))
    head_dim = w_qkv.shape[2]
    inputs_f = layer_input.astype(jnp.float32)
    squares = lax.psum(jnp.sum(inputs_f * inputs_f, axis=1), ("gx", "gy"))
    inv_rms = lax.rsqrt(squares / full_width + epsilon)
    row_gain = jnp.where(modality[:, None] == 1, norm_gain[1][None, :], norm_gain[0][None, :])
    scaled = inputs_f * inv_rms[:, None]
    normed = (scaled * row_gain).astype(jnp.bfloat16)
    w_full = lax.all_gather(w_qkv, "gz", axis=1, tiled=True)
    wo_full = lax.all_gather(w_out, "gz", axis=1, tiled=True)
    rows_block = w_full
    projected = jnp.einsum(
        "tc,mch->mth",
        lax.all_gather(normed, ("gx", "gy"), axis=1, tiled=True),
        rows_block,
        preferred_element_type=jnp.float32,
    )
    projected = projected.astype(jnp.bfloat16)
    queries = projected[0]
    keys_values = lax.all_gather(
        jnp.concatenate([projected[1], projected[2]], axis=1), "gz", axis=0, tiled=True
    )
    key_total = keys_values.shape[0]
    query_pos = lax.axis_index("gz") * tok_rows + jnp.arange(tok_rows, dtype=jnp.int32)
    query_span = span_index(query_pos, image_spans)
    key_block = 512
    block_count = key_total // key_block
    score_scale = 1.0 / math.sqrt(head_dim)
    block_ids = jnp.arange(block_count, dtype=jnp.int32)

    def block_scores(block_idx):
        first_key = block_idx * key_block
        kv_block = lax.dynamic_slice_in_dim(keys_values, first_key, key_block, 0)
        key_pos = first_key + jnp.arange(key_block, dtype=jnp.int32)
        allowed = visible(query_pos, query_span, key_pos, span_index(key_pos, image_spans))
        scores = (
            lax.dot_general(
                queries,
                kv_block[:, :head_dim],
                (((1,), (1,)), ((), ())),
                preferred_element_type=jnp.float32,
            )
            * score_scale
        )
        return (kv_block, allowed, scores)

    def gather_stats(state, block_idx):
        maxima, summed = state
        kv_block, allowed, scores = block_scores(block_idx)
        new_maxima = jnp.maximum(maxima, jnp.max(jnp.where(allowed, scores, masked_low), axis=1))
        fresh = jnp.sum(jnp.where(allowed, jnp.exp(scores - new_maxima[:, None]), 0.0), axis=1)
        return ((new_maxima, summed * jnp.exp(maxima - new_maxima) + fresh), None)

    start_state = (
        jnp.full((tok_rows,), masked_low, jnp.float32),
        jnp.zeros((tok_rows,), jnp.float32),
    )
    (maxima, summed), unused = lax.scan(gather_stats, start_state, block_ids)
    lse = maxima + jnp.log(summed)

    def block_probs(block_idx):
        kv_block, allowed, scores = block_scores(block_idx)
        return (kv_block, jnp.where(allowed, jnp.exp(scores - lse[:, None]), 0.0))

    def attend(accum, block_idx):
        kv_block, attn_p = block_probs(block_idx)
        return (
            accum
            + jnp.dot(
                attn_p.astype(jnp.bfloat16),
                kv_block[:, head_dim:],
                preferred_element_type=jnp.float32,
            ),
            None,
        )

    attended_f, unused = lax.scan(attend, jnp.zeros((tok_rows, head_dim), jnp.float32), block_ids)
    attended = attended_f.astype(jnp.bfloat16)
    all_heads = lax.all_gather(attended, ("gx", "gy"), axis=1, tiled=True)
    out_rows = lax.all_to_all(wo_full, ("gx", "gy"), split_axis=1, concat_axis=0, tiled=True)
    head_total = out_rows.shape[0] // head_dim
    per_head = jnp.einsum(
        "thd,hdc->htc",
        all_heads.reshape(tok_rows, head_total, head_dim),
        out_rows.reshape(head_total, head_dim, local_width),
        preferred_element_type=jnp.float32,
    )
    per_head = lax.optimization_barrier(per_head.astype(jnp.bfloat16)).astype(jnp.float32)
    attn_out = jnp.sum(per_head, axis=0).astype(jnp.bfloat16)
    segment = lax.all_gather(grad_out, ("gx", "gy"), axis=1, tiled=True)
    d_accum = lax.dot_general(
        segment, wo_full, (((1,), (1,)), ((), ())), preferred_element_type=jnp.float32
    )
    partial_value = lax.dot_general(
        attended, segment, (((0,), (0,)), ((), ())), preferred_element_type=jnp.float32
    )
    d_attended = d_accum.astype(jnp.bfloat16)
    row_dots = jnp.sum(d_attended.astype(jnp.float32) * attended.astype(jnp.float32), axis=1)

    def backward_block(d_query, block_idx):
        kv_block, attn_p = block_probs(block_idx)
        d_probs = lax.dot_general(
            d_attended,
            kv_block[:, head_dim:],
            (((1,), (1,)), ((), ())),
            preferred_element_type=jnp.float32,
        )
        d_scores = (attn_p * (d_probs - row_dots[:, None]) * score_scale).astype(jnp.bfloat16)
        d_query = d_query + jnp.dot(
            d_scores, kv_block[:, :head_dim], preferred_element_type=jnp.float32
        )
        d_keys = lax.dot_general(
            d_scores, queries, (((0,), (0,)), ((), ())), preferred_element_type=jnp.float32
        )
        d_values = lax.dot_general(
            attn_p.astype(jnp.bfloat16),
            d_attended,
            (((0,), (0,)), ((), ())),
            preferred_element_type=jnp.float32,
        )
        return (d_query, jnp.concatenate([d_keys, d_values], axis=1))

    d_query_f, kv_parts = lax.scan(
        backward_block, jnp.zeros((tok_rows, head_dim), jnp.float32), block_ids
    )
    kv_grad = lax.psum_scatter(
        kv_parts.reshape(key_total, 2 * head_dim).astype(jnp.bfloat16),
        "gz",
        scatter_dimension=0,
        tiled=True,
    ).astype(jnp.float32)
    grads = jnp.stack(
        [
            d_query_f.astype(jnp.bfloat16),
            kv_grad[:, :head_dim].astype(jnp.bfloat16),
            kv_grad[:, head_dim:].astype(jnp.bfloat16),
        ]
    )
    w_grad = jnp.einsum(
        "tc,mth->mch",
        lax.all_gather(normed, ("gx", "gy"), axis=1, tiled=True),
        grads,
        preferred_element_type=jnp.float32,
    )
    grad_qkv, grad_wout = (
        lax.psum_scatter(w_grad.astype(jnp.bfloat16), "gz", scatter_dimension=1, tiled=True).astype(
            jnp.float32
        ),
        lax.psum_scatter(
            partial_value.astype(jnp.bfloat16), "gz", scatter_dimension=1, tiled=True
        ).astype(jnp.float32),
    )
    rows_block = w_full
    grad_normed = (
        lax.psum_scatter(
            jnp.einsum("mch,mth->ct", rows_block, grads, preferred_element_type=jnp.float32).astype(
                jnp.bfloat16
            ),
            ("gx", "gy"),
            scatter_dimension=0,
            tiled=True,
        )
        .astype(jnp.float32)
        .T
    )
    upstream = grad_normed * row_gain
    norm_dots = lax.psum(jnp.sum(upstream * scaled, axis=1), ("gx", "gy"))
    grad_in = (inv_rms[:, None] * (upstream - scaled * (norm_dots / full_width)[:, None])).astype(
        jnp.bfloat16
    )
    onehot = (modality[:, None] == jnp.arange(2, dtype=jnp.int32)[None, :]).astype(jnp.float32)
    local_gain = jnp.dot(onehot.T, grad_normed * scaled, precision=lax.Precision.HIGHEST)
    grad_gain = lax.psum(local_gain, "gz")
    return (attn_out, grad_in, grad_qkv, grad_wout, grad_gain)


def solution(mesh):
    in_specs = (
        P("gz", ("gx", "gy")),
        P("gz"),
        P(),
        P(None, ("gx", "gy")),
        P(None, "gz", ("gx", "gy")),
        P(("gx", "gy"), "gz"),
        P("gz", ("gx", "gy")),
    )
    out_specs = (
        P("gz", ("gx", "gy")),
        P("gz", ("gx", "gy")),
        P(None, "gz", ("gx", "gy")),
        P(("gx", "gy"), "gz"),
        P(None, ("gx", "gy")),
    )
    return jax.shard_map(
        per_device, mesh=mesh, in_specs=in_specs, out_specs=out_specs, check_vma=False
    )
```

profile of v0, /device:TPU:0, one launch (start us, length us, event | category | flops | bytes accessed | tf_op | source)
XLA Modules:
  0.0 420.7 jit_solution(4267195177550142330)
XLA Ops:
  10.2 35.2 %psum.21 = f32[512]{0:T(512)S(1)} all-reduce(f32[512]{0:T(512)S(1)} %fusion.65), channel_id=1, replica_groups=mesh['gx'=4,'gy'=4,'gz'=2] {'gx','gy'}, use_global_device_ids=true, to_apply=%region_1.0 | all-reduce | flops 512 | bytes 4096 | tf_op jit(solution)/shard_map/psum | solution.py:30
  48.3 9.5 %all-gather.8.cloned.1.call-done = bf16[3,4096,128]{1,2,0:T(8,128)(2,1)} async-done(((bf16[3,2048,128]{1,2,0:T(8,128)(2,1)}), bf16[3,4096,128]{1,2,0:T(8,128)(2,1)}) %all-gather.8.cloned.1.call-update) | async-done | bytes 3145744 | tf_op jit(solution)/shard_map/all_gather | solution.py:35
  57.8 55.2 %all-gather.6.cloned.1.call-done = bf16[512,4096]{1,0:T(8,128)(2,1)} async-done(((bf16[512,256]{1,0:T(8,128)(2,1)}), bf16[512,4096]{1,0:T(8,128)(2,1)}) %all-gather.6.cloned.1.call-update) | async-done | bytes 4194320 | tf_op jit(solution)/shard_map/all_gather | solution.py:40
  113.0 5.0 %fusion.75 = f32[512,384]{0,1:S(1)} fusion(bf16[512,4096]{1,0:T(8,128)(2,1)} %all-gather.6.cloned.1.call-done, bf16[4096,384]{0,1:T(8,128)(2,1)} %bitcast.156), kind=kOutput, calls=%fused_computation.134 | convolution fusion | flops 1610612736 | bytes 8126464
  118.1 13.9 %all_gather.21 = bf16[1024,256]{0,1:T(8,128)(2,1)S(1)} all-gather(bf16[512,256]{0,1:T(8,128)(2,1)S(1)} %pad_maximum_fusion.1), channel_id=1, replica_groups=mesh['gx'=4,'gy'=4,'gz'=2] {'gz'}, dimensions={0}, use_global_device_ids=true | all-gather | bytes 786432 | tf_op jit(solution)/shard_map/all_gather | solution.py:46
  132.4 4.8 %while.43 = (s32[]{:T(128)}, f32[512]{0:T(512)S(1)}, f32[512]{0:T(512)S(1)}, s32[2]{0:T(128)S(1)}, s32[512]{0:T(512)S(1)}, /*index=5*/s32[2,8]{1,0:T(2,128)S(1)}...) while((s32[]{:T(128)}, f32[512]{0:T(512)S(1)}, ...), condition=%wide.region_7.8_spmd.clone, body=%wide.region_3.7_spmd.clone.sunk | while | flops 70803472 | bytes 2418638 | solution.py:84
  137.7 5.9 %while.44 = (s32[]{:T(128)}, f32[512,128]{1,0:T(8,128)S(1)}, s32[2]{0:T(128)S(1)}, s32[512]{0:T(512)S(1)}, s32[2,8]{1,0:T(2,128)S(1)}, /*index=5*/bf16[1024,256]...) while((s32[]{:T(128)}, f32[512,128]{1,0:T(8,128)S(1)}, ...), condition=%wide.region_10.11_spmd.clone, body=%wide.region_8.10_spmd.clone.sunk | while | flops 136467984 | bytes 945628 | solution.py:103
  143.8 47.6 %all-gather.14.cloned.1.call-done = bf16[512,4096]{1,0:T(8,128)(2,1)} async-done(((bf16[512,256]{1,0:T(8,128)(2,1)}), bf16[512,4096]{1,0:T(8,128)(2,1)}) %all-gather.14.cloned.1.call-update) | async-done | bytes 4194320 | tf_op jit(solution)/shard_map/all_gather | solution.py:116
  191.3 4.0 multiply_reduce_fusion
  196.0 9.3 %while.45 = (s32[]{:T(128)}, f32[512,128]{1,0:T(8,128)S(1)}, bf16[2,512,256]{1,2,0:T(8,128)(2,1)S(1)}, s32[2]{0:T(128)}, s32[512]{0:T(512)S(1)}, /*index=5*/s32[...) while((s32[]{:T(128)}, f32[512,128]{1,0:T(8,128)S(1)}, ...), condition=%wide.region_15.16_spmd.clone, body=%wide.region_13.15_spmd.clone.sunk | while | flops 339367424 | bytes 6974985 | solution.py:149
  206.4 3.9 convolution_convert_fusion.1
  211.1 8.2 %reduce-scatter.5.cloned.1.call-done = bf16[512,256]{1,0:T(8,128)(2,1)} async-done(((bf16[1024,256]{1,0:T(8,128)(2,1)}), bf16[512,256]{1,0:T(8,128)(2,1)}) %reduce-scatter.5.cloned.1.call-update) | async-done | bytes 262160 | tf_op jit(solution)/shard_map/reduce_scatter | solution.py:152
  220.2 5.8 %fusion.52 = bf16[4096,512]{0,1:T(8,128)(2,1)} fusion(bf16[3,4096,128]{1,2,0:T(8,128)(2,1)} %all-gather.8.cloned.1.call-done, bf16[1,512,128]{2,1,0:T(8,128)(2,1)S(1)} %get-tuple-element.678, bf16[1,512,128]{2,1,0:T(8,128)(2,1)S(1)} %get-tuple-element.677, bf16[1,512,128]{2,1,0:T(8,128)(2,1)S(1)} %convert_bitcast_fusion.1), kind=kOutput, calls=%fused_computation.84 | convolution fusion | flops 1613103104 | bytes 7733248 | tf_op jit(solution)/shard_map/mch,mth->ct/dot_general | solution.py:182
  226.3 6.1 %fusion.53 = bf16[3,4096,128]{1,2,0:T(8,128)(2,1)} fusion(bf16[512,4096]{1,0:T(8,128)(2,1)} %all-gather.6.cloned.1.call-done, bf16[1,512,128]{2,1,0:T(8,128)(2,1)S(1)} %get-tuple-element.678, bf16[1,512,128]{2,1,0:T(8,128)(2,1)S(1)} %get-tuple-element.677, bf16[1,512,128]{2,1,0:T(8,128)(2,1)S(1)} %convert_bitcast_fusion.1), kind=kOutput, calls=%fused_computation.85 | convolution fusion | flops 1612578816 | bytes 7733248 | tf_op jit(solution)/shard_map/tc,mth->mch/dot_general | solution.py:165
  233.8 5.5 %all-to-all-start = ((bf16[128,16,256]{2,0,1:T(8,128)(2,1)}), bf16[128,16,256]{2,0,1:T(8,128)(2,1)S(1)}, u32[]{:S(2)}, u32[]{:S(2)}) async-start(bf16[128,16,256]{2,0,1:T(8,128)(2,1)} %copy.51), calls=%async_computation | async-start | bytes 2097152 | tf_op jit(solution)/shard_map/all_to_all | solution.py:106
  239.3 3.1 reduce-scatter.11.cloned.1.call-done
  244.5 25.8 %all-to-all-done = bf16[128,16,256]{2,0,1:T(8,128)(2,1)S(1)} async-done(((bf16[128,16,256]{2,0,1:T(8,128)(2,1)}), bf16[128,16,256]{2,0,1:T(8,128)(2,1)S(1)}, u32[]{:S(2)}, u32[]{:S(2)}) %all-to-all-start) | async-done | bytes 1048608 | tf_op jit(solution)/shard_map/all_to_all | solution.py:106
  270.3 19.1 %all-gather.10.cloned.1.call-done = bf16[512,2048]{0,1:T(8,128)(2,1)} async-done(((bf16[512,128]{0,1:T(8,128)(2,1)}), bf16[512,2048]{0,1:T(8,128)(2,1)}) %all-gather.10.cloned.1.call-update) | async-done | bytes 2097168 | tf_op jit(solution)/shard_map/all_gather | solution.py:105
  289.4 4.8 %convolution_convert_fusion.2 = bf16[16,512,256]{2,1,0:T(8,128)(2,1)} fusion(bf16[512,16,128]{0,2,1:T(8,128)(2,1)} %bitcast.147, bf16[128,16,256]{2,0,1:T(8,128)(2,1)S(1)} %all-to-all-done), kind=kOutput, calls=%fused_computation.88 | convolution fusion | flops 538968064 | bytes 7340032 | tf_op jit(solution)/shard_map/thd,hdc->htc/dot_general | solution.py:108
  294.2 3.5 reduce_sum.98
  297.8 67.0 %reduce-scatter.7.cloned.1.call-done = bf16[256,512]{0,1:T(8,128)(2,1)} async-done(((bf16[4096,512]{0,1:T(8,128)(2,1)}), bf16[256,512]{0,1:T(8,128)(2,1)}) %reduce-scatter.7.cloned.1.call-update) | async-done | bytes 262160 | tf_op jit(solution)/shard_map/reduce_scatter | solution.py:181
  366.1 30.5 %psum.22 = f32[512]{0:T(512)S(1)} all-reduce(f32[512]{0:T(512)S(1)} %fusion.59), channel_id=1, replica_groups=mesh['gx'=4,'gy'=4,'gz'=2] {'gx','gy'}, use_global_device_ids=true, to_apply=%region_19.20 | all-reduce | flops 512 | bytes 4096 | tf_op jit(solution)/shard_map/psum | solution.py:193
  398.1 5.7 %psum.23 = f32[2,256]{1,0:T(2,128)} all-reduce(f32[2,256]{1,0:T(2,128)S(1)} %fusion.63), channel_id=1, replica_groups=mesh['gx'=4,'gy'=4,'gz'=2] {'gz'}, use_global_device_ids=true, to_apply=%region_22.23 | all-reduce | flops 512 | bytes 4096 | tf_op jit(solution)/shard_map/psum | solution.py:199
  403.8 6.4 %reduce-scatter.9.cloned.1.call-done = bf16[3,2048,128]{1,2,0:T(8,128)(2,1)} async-done(((bf16[3,4096,128]{1,2,0:T(8,128)(2,1)}), bf16[3,2048,128]{1,2,0:T(8,128)(2,1)}) %reduce-scatter.9.cloned.1.call-update) | async-done | bytes 1572880 | tf_op jit(solution)/shard_map/reduce_scatter | solution.py:172
  (153 shorter events, 36.5 us)
Async XLA Ops:
  7.2 2.8 copy-start
  7.2 38.2 %copy-start.12 = (s32[512]{0:T(512)S(1)}, s32[512]{0:T(512)}, u32[]{:S(2)}) copy-start(s32[512]{0:T(512)} %param.14) | copy-start | bytes 6148
  7.2 38.2 %copy-start.14 = (f32[2,256]{1,0:T(2,128)S(1)}, f32[2,256]{1,0:T(2,128)}, u32[]{:S(2)}) copy-start(f32[2,256]{1,0:T(2,128)} %param.16) | copy-start | bytes 6148
  7.2 39.2 %copy-start.4 = (bf16[128,2048]{1,0:T(8,128)(2,1)S(1)}, bf16[128,2048]{1,0:T(8,128)(2,1)}, u32[]{:S(2)}) copy-start(bf16[128,2048]{1,0:T(8,128)(2,1)} %param.18) | copy-start | bytes 1572868
  7.2 41.0 %copy-start.5 = (s32[2,8]{1,0:T(2,128)S(1)}, s32[2,8]{1,0:T(2,128)}, u32[]{:S(2)}) copy-start(s32[2,8]{1,0:T(2,128)} %param.15) | copy-start | bytes 196
  7.2 50.6 %all-gather.8.cloned.1.call-start = ((), (), s32[]{:S(2)}) async-start(), calls=%async_computation.6 | async-start | bytes 4718592 | tf_op jit(solution)/shard_map/all_gather | solution.py:35
  10.0 103.0 %all-gather.6.cloned.1.call-start = ((), (), s32[]{:S(2)}) async-start(), calls=%async_computation.5 | async-start | bytes 4456448 | tf_op jit(solution)/shard_map/all_gather | solution.py:40
  45.4 2.8 copy-start.10
  45.4 72.6 %copy-start.6 = (f32[1,256]{1,0:T(1,128)}, f32[1,256]{1,0:T(1,128)S(1)}, u32[]{:S(2)}) copy-start(f32[1,256]{1,0:T(1,128)S(1)} %get-tuple-element.679) | copy-start | bytes 3076
  46.3 97.4 %all-gather.12.cloned.1.call-start = ((), (), s32[]{:S(2)}) async-start(), calls=%async_computation.8 | async-start | bytes 1572864 | tf_op jit(solution)/shard_map/all_gather | solution.py:36
  47.4 143.9 %all-gather.14.cloned.1.call-start = ((), (), s32[]{:S(2)}) async-start(), calls=%async_computation.9 | async-start | bytes 4456448 | tf_op jit(solution)/shard_map/all_gather | solution.py:116
  48.0 171.2 %reduce-scatter.5.cloned.1.call-start = ((), (), s32[]{:S(2)}) async-start(), calls=%async_computation.10 | async-start | bytes 786432 | tf_op jit(solution)/shard_map/reduce_scatter | solution.py:152
  143.7 62.6 %copy-start.2 = (bf16[512,128]{0,1:T(8,128)(2,1)}, bf16[512,128]{0,1:T(8,128)(2,1)S(1)}, u32[]{:S(2)}) copy-start(bf16[512,128]{0,1:T(8,128)(2,1)S(1)} %copy.49) | copy-start | bytes 393220
  206.3 36.1 %reduce-scatter.11.cloned.1.call-start = ((), (), s32[]{:S(2)}) async-start(), calls=%async_computation.13 | async-start | bytes 1572864 | tf_op jit(solution)/shard_map/reduce_scatter | solution.py:175
  210.3 79.1 %all-gather.10.cloned.1.call-start = ((), (), s32[]{:S(2)}) async-start(), calls=%async_computation.7 | async-start | bytes 2228224 | tf_op jit(solution)/shard_map/all_gather | solution.py:105
  211.0 153.8 %reduce-scatter.7.cloned.1.call-start = ((), (), s32[]{:S(2)}) async-start(), calls=%async_computation.11 | async-start | bytes 4456448 | tf_op jit(solution)/shard_map/reduce_scatter | solution.py:181
  226.1 6.4 %copy-start.1 = (bf16[128,4096]{0,1:T(8,128)(2,1)S(1)}, bf16[128,4096]{0,1:T(8,128)(2,1)}, u32[]{:S(2)}) copy-start(bf16[128,4096]{0,1:T(8,128)(2,1)} %all-gather.12.cloned.1.call-done) | copy-start | bytes 3145732
  226.1 184.1 %reduce-scatter.9.cloned.1.call-start = ((), (), s32[]{:S(2)}) async-start(), calls=%async_computation.12 | async-start | bytes 4718592 | tf_op jit(solution)/shard_map/reduce_scatter | solution.py:172
  233.8 36.5 %all-to-all-start = ((bf16[128,16,256]{2,0,1:T(8,128)(2,1)}), bf16[128,16,256]{2,0,1:T(8,128)(2,1)S(1)}, u32[]{:S(2)}, u32[]{:S(2)}) async-start(bf16[128,16,256]{2,0,1:T(8,128)(2,1)} %copy.51), calls=%async_computation | async-start | bytes 2097152 | tf_op jit(solution)/shard_map/all_to_all | solution.py:106
  289.4 75.4 %copy-start.7 = (f32[1,256]{1,0:T(1,128)S(1)}, f32[1,256]{1,0:T(1,128)}, u32[]{:S(2)}) copy-start(f32[1,256]{1,0:T(1,128)} %copy-done.6) | copy-start | bytes 3076
  289.4 75.4 %copy-start.9 = (f32[1,256]{1,0:T(1,128)S(1)}, f32[1,256]{1,0:T(1,128)}, u32[]{:S(2)}) copy-start(f32[1,256]{1,0:T(1,128)} %copy-done.8) | copy-start | bytes 3076
  289.4 75.4 %copy-start.11 = (pred[512]{0:T(512)(128)(4,1)S(1)}, pred[512]{0:T(512)(128)(4,1)}, u32[]{:S(2)}) copy-start(pred[512]{0:T(512)(128)(4,1)} %copy-done.10) | copy-start | bytes 1540
  294.2 102.4 %copy-start.13 = (s32[512]{0:T(512)S(1)}, s32[512]{0:T(512)}, u32[]{:S(2)}) copy-start(s32[512]{0:T(512)} %param.14) | copy-start | bytes 6148
  364.8 48.5 %copy-start.3 = (bf16[256,512]{0,1:T(8,128)(2,1)S(1)}, bf16[256,512]{0,1:T(8,128)(2,1)}, u32[]{:S(2)}) copy-start(bf16[256,512]{0,1:T(8,128)(2,1)} %reduce-scatter.7.cloned.1.call-done) | copy-start | bytes 786436
  (1 other events, 2.7 us)
Sparse Core Ops, SparseCore 0:
  10.1 47.6 all-gather.7
  60.5 52.4 all-gather.5
  115.1 23.5 all-gather.11
  140.6 50.6 all-gather.13
  206.4 12.7 reduce-scatter.4
  221.9 20.3 reduce-scatter.10
  245.1 44.2 all-gather.9
  293.3 71.4 reduce-scatter.6
  367.6 42.5 reduce-scatter.8
where the time goes:
time: 421 us
  waiting for transfers between devices  243 us (58%)
  blocking collectives  85.3 us (20%)
  matrix products  40.2 us (10%)
  local copies, waits for them, and re-layouts  16.1 us (4%)
  between operations  14.2 us (3%)
  other arithmetic  11.5 us (3%)
  starting transfers between devices  6.02 us (1%)
  loops' own time  4.31 us (1%)
    reduce_scatter x1, waiting for transfers between devices, per_device(): lax.psum_scatter(jnp.einsum('mch,mth->ct', rows_block, grads, preferred_e...  67 us
    all_gather x1, waiting for transfers between devices, per_device(): lax.all_gather(normed, ('gx', 'gy'), axis=1, tiled=True)  55.2 us
    all_gather x1, waiting for transfers between devices, per_device(): segment = lax.all_gather(grad_out, ('gx', 'gy'), axis=1, tiled=True)  47.6 us
    psum x1, blocking collectives, per_device(): squares = lax.psum(jnp.sum(inputs_f * inputs_f, axis=1), ('gx', 'gy'))  35.2 us
    psum x1, blocking collectives, per_device(): norm_dots = lax.psum(jnp.sum(upstream * scaled, axis=1), ('gx', 'gy'))  30.5 us
    all_to_all x1, waiting for transfers between devices, per_device(): lax.all_to_all(wo_full, ('gx', 'gy'), split_axis=1, concat_axis=0, tiled=...  25.8 us
    all_gather x1, waiting for transfers between devices, per_device(): all_heads = lax.all_gather(attended, ('gx', 'gy'), axis=1, tiled=True)  19.1 us
    all_gather x1, blocking collectives, per_device(): lax.all_gather(jnp.concatenate([projected[1], projected[2]], axis=1), 'gz...  13.9 us
  transfers between devices with their start and end apart: 10, of which 9 were waited for; matrix products, arithmetic and copies ran while one was open for 11% of the time, Pallas kernels for 0%

commit v1 on v0

--- a/solution.py
+++ b/solution.py
@@ -27,7 +27,7 @@
     full_width = local_width * lax.axis_size(("gx", "gy"))
     head_dim = w_qkv.shape[2]
     inputs_f = layer_input.astype(jnp.float32)
-    squares = lax.psum(jnp.sum(inputs_f * inputs_f, axis=1), ("gx", "gy"))
+    squares = jax.lax.all_gather(jnp.sum(inputs_f * inputs_f, axis=1), ("gx", "gy")).sum(axis=0)
     inv_rms = lax.rsqrt(squares / full_width + epsilon)
     row_gain = jnp.where(modality[:, None] == 1, norm_gain[1][None, :], norm_gain[0][None, :])
     scaled = inputs_f * inv_rms[:, None]

time: 421 us -> 421 us (level)
    psum x1 -> x0, blocking collectives: 35.2 us -> none  [per_device(): squares = lax.psum(jnp.sum(inputs_f * inputs_f, axis=1), ('gx', 'gy'))]
    all_gather x0 -> x1, blocking collectives: none -> 34.1 us  [per_device(): jax.lax.all_gather(jnp.sum(inputs_f * inputs_f, axis=1), ('gx', 'gy'))]
where the time goes in v1:
time: 421 us
  waiting for transfers between devices  244 us (58%)
  blocking collectives  84.2 us (20%)
  matrix products  40.2 us (10%)
  local copies, waits for them, and re-layouts  16.1 us (4%)
  between operations  14.2 us (3%)
  other arithmetic  11.5 us (3%)
  starting transfers between devices  6.02 us (1%)
  loops' own time  4.31 us (1%)
    reduce_scatter x1, waiting for transfers between devices, per_device(): lax.psum_scatter(jnp.einsum('mch,mth->ct', rows_block, grads, preferred_e...  67 us
    all_gather x1, waiting for transfers between devices, per_device(): lax.all_gather(normed, ('gx', 'gy'), axis=1, tiled=True)  55.2 us
    all_gather x1, waiting for transfers between devices, per_device(): segment = lax.all_gather(grad_out, ('gx', 'gy'), axis=1, tiled=True)  47.6 us
    all_gather x1, blocking collectives, per_device(): jax.lax.all_gather(jnp.sum(inputs_f * inputs_f, axis=1), ('gx', 'gy'))  34.1 us
    psum x1, blocking collectives, per_device(): norm_dots = lax.psum(jnp.sum(upstream * scaled, axis=1), ('gx', 'gy'))  30.5 us
    all_to_all x1, waiting for transfers between devices, per_device(): lax.all_to_all(wo_full, ('gx', 'gy'), split_axis=1, concat_axis=0, tiled=...  25.8 us
    all_gather x1, waiting for transfers between devices, per_device(): all_heads = lax.all_gather(attended, ('gx', 'gy'), axis=1, tiled=True)  19.1 us
    all_gather x1, blocking collectives, per_device(): lax.all_gather(jnp.concatenate([projected[1], projected[2]], axis=1), 'gz...  13.9 us
  transfers between devices with their start and end apart: 10, of which 9 were waited for; matrix products, arithmetic and copies ran while one was open for 11% of the time, Pallas kernels for 0%

profile of v1, /device:TPU:0, one launch (start us, length us, event | category | flops | bytes accessed | tf_op | source)
XLA Modules:
  0.0 420.7 jit_solution(6988923968176401827)
XLA Ops:
  10.2 34.1 %all-gather.1 = f32[16,1,512]{2,1,0:T(1,128)S(1)} all-gather(f32[1,1,512]{2,1,0:T(1,128)S(1)} %bitcast.157), channel_id=2, replica_groups=mesh['gx'=4,'gy'=4,'gz'=2] {'gx','gy'}, dimensions={0}, use_global_device_ids=true | all-gather | bytes 34816 | tf_op jit(solution)/shard_map/all_gather | solution.py:30
  47.2 10.6 %all-gather.10.cloned.1.call-done = bf16[3,4096,128]{1,2,0:T(8,128)(2,1)} async-done(((bf16[3,2048,128]{1,2,0:T(8,128)(2,1)}), bf16[3,4096,128]{1,2,0:T(8,128)(2,1)}) %all-gather.10.cloned.1.call-update) | async-done | bytes 3145744 | tf_op jit(solution)/shard_map/all_gather | solution.py:35
  57.8 55.2 %all-gather.8.cloned.1.call-done = bf16[512,4096]{1,0:T(8,128)(2,1)} async-done(((bf16[512,256]{1,0:T(8,128)(2,1)}), bf16[512,4096]{1,0:T(8,128)(2,1)}) %all-gather.8.cloned.1.call-update) | async-done | bytes 4194320 | tf_op jit(solution)/shard_map/all_gather | solution.py:40
  113.0 5.0 %fusion.75 = f32[512,384]{0,1:S(1)} fusion(bf16[512,4096]{1,0:T(8,128)(2,1)} %all-gather.8.cloned.1.call-done, bf16[4096,384]{0,1:T(8,128)(2,1)} %bitcast.158), kind=kOutput, calls=%fused_computation.134 | convolution fusion | flops 1610612736 | bytes 8126464
  118.1 13.9 %all_gather.29 = bf16[1024,256]{0,1:T(8,128)(2,1)S(1)} all-gather(bf16[512,256]{0,1:T(8,128)(2,1)S(1)} %pad_maximum_fusion.1), channel_id=1, replica_groups=mesh['gx'=4,'gy'=4,'gz'=2] {'gz'}, dimensions={0}, use_global_device_ids=true | all-gather | bytes 786432 | tf_op jit(solution)/shard_map/all_gather | solution.py:46
  132.4 4.8 %while.43 = (s32[]{:T(128)}, f32[512]{0:T(512)S(1)}, f32[512]{0:T(512)S(1)}, s32[2]{0:T(128)S(1)}, s32[512]{0:T(512)S(1)}, /*index=5*/s32[2,8]{1,0:T(2,128)S(1)}...) while((s32[]{:T(128)}, f32[512]{0:T(512)S(1)}, ...), condition=%wide.region_7.8_spmd.clone, body=%wide.region_3.7_spmd.clone.sunk | while | flops 70803472 | bytes 2418638 | solution.py:84
  137.7 5.9 %while.44 = (s32[]{:T(128)}, f32[512,128]{1,0:T(8,128)S(1)}, s32[2]{0:T(128)S(1)}, s32[512]{0:T(512)S(1)}, s32[2,8]{1,0:T(2,128)S(1)}, /*index=5*/bf16[1024,256]...) while((s32[]{:T(128)}, f32[512,128]{1,0:T(8,128)S(1)}, ...), condition=%wide.region_10.11_spmd.clone, body=%wide.region_8.10_spmd.clone.sunk | while | flops 136467984 | bytes 945628 | solution.py:103
  143.8 47.6 %all-gather.16.cloned.1.call-done = bf16[512,4096]{1,0:T(8,128)(2,1)} async-done(((bf16[512,256]{1,0:T(8,128)(2,1)}), bf16[512,4096]{1,0:T(8,128)(2,1)}) %all-gather.16.cloned.1.call-update) | async-done | bytes 4194320 | tf_op jit(solution)/shard_map/all_gather | solution.py:116
  191.3 4.0 multiply_reduce_fusion
  196.0 9.3 %while.45 = (s32[]{:T(128)}, f32[512,128]{1,0:T(8,128)S(1)}, bf16[2,512,256]{1,2,0:T(8,128)(2,1)S(1)}, s32[2]{0:T(128)}, s32[512]{0:T(512)S(1)}, /*index=5*/s32[...) while((s32[]{:T(128)}, f32[512,128]{1,0:T(8,128)S(1)}, ...), condition=%wide.region_15.16_spmd.clone, body=%wide.region_13.15_spmd.clone.sunk | while | flops 339367424 | bytes 6974985 | solution.py:149
  206.4 3.9 convolution_convert_fusion.1
  211.1 8.2 %reduce-scatter.5.cloned.1.call-done = bf16[512,256]{1,0:T(8,128)(2,1)} async-done(((bf16[1024,256]{1,0:T(8,128)(2,1)}), bf16[512,256]{1,0:T(8,128)(2,1)}) %reduce-scatter.5.cloned.1.call-update) | async-done | bytes 262160 | tf_op jit(solution)/shard_map/reduce_scatter | solution.py:152
  220.2 5.8 %fusion.52 = bf16[4096,512]{0,1:T(8,128)(2,1)} fusion(bf16[3,4096,128]{1,2,0:T(8,128)(2,1)} %all-gather.10.cloned.1.call-done, bf16[1,512,128]{2,1,0:T(8,128)(2,1)S(1)} %get-tuple-element.713, bf16[1,512,128]{2,1,0:T(8,128)(2,1)S(1)} %get-tuple-element.712, bf16[1,512,128]{2,1,0:T(8,128)(2,1)S(1)} %convert_bitcast_fusion.1), kind=kOutput, calls=%fused_computation.84 | convolution fusion | flops 1613103104 | bytes 7733248 | tf_op jit(solution)/shard_map/mch,mth->ct/dot_general | solution.py:182
  226.3 6.1 %fusion.53 = bf16[3,4096,128]{1,2,0:T(8,128)(2,1)} fusion(bf16[512,4096]{1,0:T(8,128)(2,1)} %all-gather.8.cloned.1.call-done, bf16[1,512,128]{2,1,0:T(8,128)(2,1)S(1)} %get-tuple-element.713, bf16[1,512,128]{2,1,0:T(8,128)(2,1)S(1)} %get-tuple-element.712, bf16[1,512,128]{2,1,0:T(8,128)(2,1)S(1)} %convert_bitcast_fusion.1), kind=kOutput, calls=%fused_computation.85 | convolution fusion | flops 1612578816 | bytes 7733248 | tf_op jit(solution)/shard_map/tc,mth->mch/dot_general | solution.py:165
  233.8 5.5 %all-to-all-start = ((bf16[128,16,256]{2,0,1:T(8,128)(2,1)}), bf16[128,16,256]{2,0,1:T(8,128)(2,1)S(1)}, u32[]{:S(2)}, u32[]{:S(2)}) async-start(bf16[128,16,256]{2,0,1:T(8,128)(2,1)} %copy.68), calls=%async_computation | async-start | bytes 2097152 | tf_op jit(solution)/shard_map/all_to_all | solution.py:106
  239.3 3.1 reduce-scatter.11.cloned.1.call-done
  244.5 25.8 %all-to-all-done = bf16[128,16,256]{2,0,1:T(8,128)(2,1)S(1)} async-done(((bf16[128,16,256]{2,0,1:T(8,128)(2,1)}), bf16[128,16,256]{2,0,1:T(8,128)(2,1)S(1)}, u32[]{:S(2)}, u32[]{:S(2)}) %all-to-all-start) | async-done | bytes 1048608 | tf_op jit(solution)/shard_map/all_to_all | solution.py:106
  270.3 19.1 %all-gather.12.cloned.1.call-done = bf16[512,2048]{0,1:T(8,128)(2,1)} async-done(((bf16[512,128]{0,1:T(8,128)(2,1)}), bf16[512,2048]{0,1:T(8,128)(2,1)}) %all-gather.12.cloned.1.call-update) | async-done | bytes 2097168 | tf_op jit(solution)/shard_map/all_gather | solution.py:105
  289.4 4.8 %convolution_convert_fusion.2 = bf16[16,512,256]{2,1,0:T(8,128)(2,1)} fusion(bf16[512,16,128]{0,2,1:T(8,128)(2,1)} %bitcast.148, bf16[128,16,256]{2,0,1:T(8,128)(2,1)S(1)} %all-to-all-done), kind=kOutput, calls=%fused_computation.88 | convolution fusion | flops 538968064 | bytes 7340032 | tf_op jit(solution)/shard_map/thd,hdc->htc/dot_general | solution.py:108
  294.2 3.5 reduce_sum.108
  297.8 67.0 %reduce-scatter.7.cloned.1.call-done = bf16[256,512]{0,1:T(8,128)(2,1)} async-done(((bf16[4096,512]{0,1:T(8,128)(2,1)}), bf16[256,512]{0,1:T(8,128)(2,1)}) %reduce-scatter.7.cloned.1.call-update) | async-done | bytes 262160 | tf_op jit(solution)/shard_map/reduce_scatter | solution.py:181
  366.1 30.5 %psum.14 = f32[512]{0:T(512)S(1)} all-reduce(f32[512]{0:T(512)S(1)} %fusion.59), channel_id=1, replica_groups=mesh['gx'=4,'gy'=4,'gz'=2] {'gx','gy'}, use_global_device_ids=true, to_apply=%region_19.20 | all-reduce | flops 512 | bytes 4096 | tf_op jit(solution)/shard_map/psum | solution.py:193
  398.1 5.7 %psum.15 = f32[2,256]{1,0:T(2,128)} all-reduce(f32[2,256]{1,0:T(2,128)S(1)} %fusion.63), channel_id=1, replica_groups=mesh['gx'=4,'gy'=4,'gz'=2] {'gz'}, use_global_device_ids=true, to_apply=%region_22.23 | all-reduce | flops 512 | bytes 4096 | tf_op jit(solution)/shard_map/psum | solution.py:199
  403.8 6.4 %reduce-scatter.9.cloned.1.call-done = bf16[3,2048,128]{1,2,0:T(8,128)(2,1)} async-done(((bf16[3,4096,128]{1,2,0:T(8,128)(2,1)}), bf16[3,2048,128]{1,2,0:T(8,128)(2,1)}) %reduce-scatter.9.cloned.1.call-update) | async-done | bytes 1572880 | tf_op jit(solution)/shard_map/reduce_scatter | solution.py:172
  (154 shorter events, 36.5 us)
Async XLA Ops:
  7.2 2.8 copy-start
  7.2 37.1 %copy-start.12 = (s32[512]{0:T(512)S(1)}, s32[512]{0:T(512)}, u32[]{:S(2)}) copy-start(s32[512]{0:T(512)} %param.14) | copy-start | bytes 6148
  7.2 37.1 %copy-start.14 = (f32[2,256]{1,0:T(2,128)S(1)}, f32[2,256]{1,0:T(2,128)}, u32[]{:S(2)}) copy-start(f32[2,256]{1,0:T(2,128)} %param.16) | copy-start | bytes 6148
  7.2 38.2 %copy-start.4 = (bf16[128,2048]{1,0:T(8,128)(2,1)S(1)}, bf16[128,2048]{1,0:T(8,128)(2,1)}, u32[]{:S(2)}) copy-start(bf16[128,2048]{1,0:T(8,128)(2,1)} %param.18) | copy-start | bytes 1572868
  7.2 39.9 %copy-start.5 = (s32[2,8]{1,0:T(2,128)S(1)}, s32[2,8]{1,0:T(2,128)}, u32[]{:S(2)}) copy-start(s32[2,8]{1,0:T(2,128)} %param.15) | copy-start | bytes 196
  7.2 50.6 %all-gather.10.cloned.1.call-start = ((), (), s32[]{:S(2)}) async-start(), calls=%async_computation.6 | async-start | bytes 4718592 | tf_op jit(solution)/shard_map/all_gather | solution.py:35
  10.0 103.0 %all-gather.8.cloned.1.call-start = ((), (), s32[]{:S(2)}) async-start(), calls=%async_computation.5 | async-start | bytes 4456448 | tf_op jit(solution)/shard_map/all_gather | solution.py:40
  44.3 2.8 copy-start.10
  44.4 73.6 %copy-start.6 = (f32[1,256]{1,0:T(1,128)}, f32[1,256]{1,0:T(1,128)S(1)}, u32[]{:S(2)}) copy-start(f32[1,256]{1,0:T(1,128)S(1)} %get-tuple-element.714) | copy-start | bytes 3076
  45.3 98.4 %all-gather.14.cloned.1.call-start = ((), (), s32[]{:S(2)}) async-start(), calls=%async_computation.8 | async-start | bytes 1572864 | tf_op jit(solution)/shard_map/all_gather | solution.py:36
  46.4 144.9 %all-gather.16.cloned.1.call-start = ((), (), s32[]{:S(2)}) async-start(), calls=%async_computation.9 | async-start | bytes 4456448 | tf_op jit(solution)/shard_map/all_gather | solution.py:116
  47.0 172.3 %reduce-scatter.5.cloned.1.call-start = ((), (), s32[]{:S(2)}) async-start(), calls=%async_computation.10 | async-start | bytes 786432 | tf_op jit(solution)/shard_map/reduce_scatter | solution.py:152
  143.7 62.6 %copy-start.2 = (bf16[512,128]{0,1:T(8,128)(2,1)}, bf16[512,128]{0,1:T(8,128)(2,1)S(1)}, u32[]{:S(2)}) copy-start(bf16[512,128]{0,1:T(8,128)(2,1)S(1)} %copy.66) | copy-start | bytes 393220
  206.3 36.1 %reduce-scatter.11.cloned.1.call-start = ((), (), s32[]{:S(2)}) async-start(), calls=%async_computation.13 | async-start | bytes 1572864 | tf_op jit(solution)/shard_map/reduce_scatter | solution.py:175
  210.3 79.1 %all-gather.12.cloned.1.call-start = ((), (), s32[]{:S(2)}) async-start(), calls=%async_computation.7 | async-start | bytes 2228224 | tf_op jit(solution)/shard_map/all_gather | solution.py:105
  211.0 153.8 %reduce-scatter.7.cloned.1.call-start = ((), (), s32[]{:S(2)}) async-start(), calls=%async_computation.11 | async-start | bytes 4456448 | tf_op jit(solution)/shard_map/reduce_scatter | solution.py:181
  226.1 6.4 %copy-start.1 = (bf16[128,4096]{0,1:T(8,128)(2,1)S(1)}, bf16[128,4096]{0,1:T(8,128)(2,1)}, u32[]{:S(2)}) copy-start(bf16[128,4096]{0,1:T(8,128)(2,1)} %all-gather.14.cloned.1.call-done) | copy-start | bytes 3145732
  226.1 184.1 %reduce-scatter.9.cloned.1.call-start = ((), (), s32[]{:S(2)}) async-start(), calls=%async_computation.12 | async-start | bytes 4718592 | tf_op jit(solution)/shard_map/reduce_scatter | solution.py:172
  233.8 36.5 %all-to-all-start = ((bf16[128,16,256]{2,0,1:T(8,128)(2,1)}), bf16[128,16,256]{2,0,1:T(8,128)(2,1)S(1)}, u32[]{:S(2)}, u32[]{:S(2)}) async-start(bf16[128,16,256]{2,0,1:T(8,128)(2,1)} %copy.68), calls=%async_computation | async-start | bytes 2097152 | tf_op jit(solution)/shard_map/all_to_all | solution.py:106
  289.4 75.4 %copy-start.7 = (f32[1,256]{1,0:T(1,128)S(1)}, f32[1,256]{1,0:T(1,128)}, u32[]{:S(2)}) copy-start(f32[1,256]{1,0:T(1,128)} %copy-done.6) | copy-start | bytes 3076
  289.4 75.4 %copy-start.9 = (f32[1,256]{1,0:T(1,128)S(1)}, f32[1,256]{1,0:T(1,128)}, u32[]{:S(2)}) copy-start(f32[1,256]{1,0:T(1,128)} %copy-done.8) | copy-start | bytes 3076
  289.4 75.4 %copy-start.11 = (pred[512]{0:T(512)(128)(4,1)S(1)}, pred[512]{0:T(512)(128)(4,1)}, u32[]{:S(2)}) copy-start(pred[512]{0:T(512)(128)(4,1)} %copy-done.10) | copy-start | bytes 1540
  294.2 102.4 %copy-start.13 = (s32[512]{0:T(512)S(1)}, s32[512]{0:T(512)}, u32[]{:S(2)}) copy-start(s32[512]{0:T(512)} %param.14) | copy-start | bytes 6148
  364.8 48.5 %copy-start.3 = (bf16[256,512]{0,1:T(8,128)(2,1)S(1)}, bf16[256,512]{0,1:T(8,128)(2,1)}, u32[]{:S(2)}) copy-start(bf16[256,512]{0,1:T(8,128)(2,1)} %reduce-scatter.7.cloned.1.call-done) | copy-start | bytes 786436
  (1 other events, 2.7 us)
Sparse Core Ops, SparseCore 0:
  10.1 47.6 all-gather.9
  60.5 52.4 all-gather.7
  115.1 23.5 all-gather.13
  140.6 50.6 all-gather.15
  206.4 12.7 reduce-scatter.4
  221.9 20.3 reduce-scatter.10
  245.1 44.2 all-gather.11
  293.3 71.4 reduce-scatter.6
  367.6 42.5 reduce-scatter.8
